TPU v7x, 32 devices: a whole 2x2x4 slice. The times are simulated.
32 devices in a mesh: replica: 2 (over x), data2: 4 (over z), data: 4 (over y, core).
Axes of the slice: x: 2, y: 2, z: 4, core: 2. Of those that a mesh axis runs over, the one named last changes fastest.
Arguments:
- query_hidden: bfloat16 [256, 32, 768], P(('replica', 'data2', 'data')), parts along dimension 0
- doc_hidden: bfloat16 [256, 300, 768], P(('replica', 'data2', 'data')), parts along dimension 0
- w_proj: bfloat16 [768, 128], replicated
- query_mask: int32 [256, 32], P(('replica', 'data2', 'data')), parts along dimension 0
- doc_mask: int32 [256, 300], P(('replica', 'data2', 'data')), parts along dimension 0
- temperature: float32 [], replicated
Outputs:
- output 1: float32 [256], P(('replica', 'data2', 'data')), parts along dimension 0
- output 2: float32 [2], P('replica'), parts along dimension 0
There are 2 independent parts. A program takes and returns all parts, laid end to end along the dimension named above; an argument that names none is the same for every part.
All inputs are finite; a program needn't handle non-finite values.
Results may differ from a plain program's by a relative error of at most 0.001.
Values are sent between devices in bfloat16 or wider.
A program may use at most 1 GiB of HBM per device.

v0:
```python
import jax
import jax.numpy as jnp
from jax import lax
from jax.sharding import PartitionSpec as P


def project_norm(hidden, w_proj):
    projected = jnp.einsum('bld,de->ble', hidden, w_proj, preferred_element_type=jnp.float32)
    norm_len = jnp.sqrt(jnp.sum(projected * projected, axis=-1, keepdims=True))
    return (projected / jnp.maximum(norm_len, 1e-12)).astype(jnp.bfloat16)


def tile_scores(q_block, p_block, doc_valid):
    similarity = jnp.einsum('qtc,jsc->qtjs', q_block, p_block, preferred_element_type=jnp.float32)
    best_match = jnp.max(jnp.where(doc_valid[None, None], similarity, -jnp.inf), axis=-1)
    return jnp.sum(best_match, axis=1)


def solution(mesh):
    outer_size = mesh.shape['data2']
    inner_size = mesh.shape['data']
    group_size = outer_size * inner_size
    batch_axes = ('data2', 'data')
    row_spec = P(('replica', 'data2', 'data'))
    tok_spec = P(('replica', 'data2', 'data'), None, None)
    mask_spec = P(('replica', 'data2', 'data'), None)

    def local_step(query_hidden, doc_hidden, w_proj, query_mask, doc_mask, value_a11):
        local_batch = query_hidden.shape[0]
        total_batch = local_batch * group_size
        q_vecs = project_norm(query_hidden, w_proj)
        q_vecs = jnp.where(query_mask[:, :, None] > 0, q_vecs, jnp.zeros_like(q_vecs))
        p_vecs = project_norm(doc_hidden, w_proj)
        doc_valid = doc_mask > 0
        q_all = lax.all_gather(q_vecs, 'data', axis=0, tiled=True)
        q_all = lax.all_gather(q_all, 'data2', axis=0, tiled=True)
        q_blocks = q_all.reshape(group_size, local_batch, q_all.shape[1], q_all.shape[2])
        column = lax.map(lambda q_block: tile_scores(q_block, p_vecs, doc_valid), q_blocks)
        column = column.reshape(outer_size, inner_size, local_batch, local_batch)
        column = lax.all_to_all(column, 'data', 1, 1, tiled=True)
        column = lax.all_to_all(column, 'data2', 0, 0, tiled=True)
        score_row = jnp.transpose(column, (2, 0, 1, 3)).reshape(local_batch, total_batch)
        logits = score_row / value_a11
        home_index = lax.axis_index('data2') * inner_size + lax.axis_index('data')
        own_logits = lax.dynamic_slice_in_dim(logits, home_index * local_batch, local_batch, axis=1)
        losses = jax.nn.logsumexp(logits, axis=1) - jnp.diagonal(own_logits)
        mean_loss = lax.psum(jnp.sum(losses), batch_axes) / total_batch
        return losses, mean_loss.reshape(1)

    return jax.shard_map(local_step, mesh=mesh, in_specs=(tok_spec, tok_spec, P(None, None), mask_spec, mask_spec, P()), out_specs=(row_spec, P('replica')), check_vma=False)
```

profile of v0, /device:TPU:0, one launch (start us, length us, event | category | flops | bytes accessed | tf_op | source)
XLA Modules:
  0.0 131.4 jit_solution(8300723265911455217)
XLA Ops:
  7.2 0.9 copy-done
  8.2 1.2 multiply_reduce_fusion.1
  9.4 0.7 broadcast_compare_fusion.1
  10.3 7.3 %all_gather.6 = bf16[32,32,128]{2,1,0:T(8,128)(2,1)} all-gather(bf16[8,32,128]{2,1,0:T(8,128)(2,1)S(1)} %fusion.8), channel_id=1, replica_groups=mesh['replica'=2,'data2'=4,'data'=4] {'data'}, dimensions={0}, use_global_device_ids=true | all-gather | bytes 327680 | tf_op jit(solution)/shard_map/all_gather | solution.py:35
  17.6 3.3 %multiply_reduce_fusion = (f32[8,300]{0,1:T(8,128)S(1)}, f32[8,300,128]{2,0,1:T(8,128)S(1)}) fusion(bf16[8,300,768]{2,0,1:T(8,128)(2,1)} %param.9, bf16[768,128]{1,0:T(8,128)(2,1)} %param.10), kind=kOutput, calls=%fused_computation.8 | convolution fusion | flops 472471200 | bytes 5121408 | tf_op jit(solution)/shard_map/bld,de->ble/dot_general | solution.py:8
  21.4 25.4 %all-gather.2.cloned.1.call-done = bf16[128,32,128]{2,1,0:T(8,128)(2,1)} async-done(((bf16[32,32,128]{2,1,0:T(8,128)(2,1)}), bf16[128,32,128]{2,1,0:T(8,128)(2,1)}) %all-gather.2.cloned.1.call-update) | async-done | bytes 1048592 | tf_op jit(solution)/shard_map/all_gather | solution.py:36
  46.9 25.4 %while.10 = (s32[]{:T(128)}, f32[16,8,8]{2,1,0:T(8,128)S(1)}, pred[8,300]{1,0:T(8,128)(4,1)S(1)}, bf16[16,8,32,128]{3,2,1,0:T(8,128)(2,1)}, bf16[8,300,128]{2,1,0:T(8,128)(2,1)S(1)}, /*index=5*/s32[]{:T(128)}, f32[]{:T(128)}) while((s32[]{:T(128)}, f32[16,8,8]{2,1,0:T(8,128)S(1)}, pred[8,300]{1,0:T(8,128)(4,1)S(1)}, ...), condition=%wide.region_5.6_spmd, body=%wide.region_2.5_spmd.sunk | while | flops 158515136 | bytes 707765 | solution.py:38
  46.9 1.5 %select_reduce_fusion.2 = f32[8,32,8]{1,2,0:T(8,128)S(1)} fusion(pred[8,300]{1,0:T(8,128)(4,1)S(1)} %get-tuple-element.105, bf16[8,300,128]{2,1,0:T(8,128)(2,1)S(1)} %get-tuple-element.107, bf16[16,8,32,128]{3,2,1,0:T(8,128)(2,1)} %get-tuple-element.106, s32[]{:T(128)} %get-tuple-element.96), kind=kOutput, calls=%fused_computation.1.clone.1 | convolution fusion | flops 158513152 | bytes 691040 | tf_op jit(solution)/shard_map/while/body/eval_jaxpr/qtc,jsc->qtjs/dot_general | solution.py:14
  48.5 1.5 %select_reduce_fusion.2 = f32[8,32,8]{1,2,0:T(8,128)S(1)} fusion(pred[8,300]{1,0:T(8,128)(4,1)S(1)} %get-tuple-element.105, bf16[8,300,128]{2,1,0:T(8,128)(2,1)S(1)} %get-tuple-element.107, bf16[16,8,32,128]{3,2,1,0:T(8,128)(2,1)} %get-tuple-element.106, s32[]{:T(128)} %get-tuple-element.96), kind=kOutput, calls=%fused_computation.1.clone.1 | convolution fusion | flops 158513152 | bytes 691040 | tf_op jit(solution)/shard_map/while/body/eval_jaxpr/qtc,jsc->qtjs/dot_general | solution.py:14
  50.1 1.5 %select_reduce_fusion.2 = f32[8,32,8]{1,2,0:T(8,128)S(1)} fusion(pred[8,300]{1,0:T(8,128)(4,1)S(1)} %get-tuple-element.105, bf16[8,300,128]{2,1,0:T(8,128)(2,1)S(1)} %get-tuple-element.107, bf16[16,8,32,128]{3,2,1,0:T(8,128)(2,1)} %get-tuple-element.106, s32[]{:T(128)} %get-tuple-element.96), kind=kOutput, calls=%fused_computation.1.clone.1 | convolution fusion | flops 158513152 | bytes 691040 | tf_op jit(solution)/shard_map/while/body/eval_jaxpr/qtc,jsc->qtjs/dot_general | solution.py:14
  51.7 1.5 %select_reduce_fusion.2 = f32[8,32,8]{1,2,0:T(8,128)S(1)} fusion(pred[8,300]{1,0:T(8,128)(4,1)S(1)} %get-tuple-element.105, bf16[8,300,128]{2,1,0:T(8,128)(2,1)S(1)} %get-tuple-element.107, bf16[16,8,32,128]{3,2,1,0:T(8,128)(2,1)} %get-tuple-element.106, s32[]{:T(128)} %get-tuple-element.96), kind=kOutput, calls=%fused_computation.1.clone.1 | convolution fusion | flops 158513152 | bytes 691040 | tf_op jit(solution)/shard_map/while/body/eval_jaxpr/qtc,jsc->qtjs/dot_general | solution.py:14
  53.2 1.5 %select_reduce_fusion.2 = f32[8,32,8]{1,2,0:T(8,128)S(1)} fusion(pred[8,300]{1,0:T(8,128)(4,1)S(1)} %get-tuple-element.105, bf16[8,300,128]{2,1,0:T(8,128)(2,1)S(1)} %get-tuple-element.107, bf16[16,8,32,128]{3,2,1,0:T(8,128)(2,1)} %get-tuple-element.106, s32[]{:T(128)} %get-tuple-element.96), kind=kOutput, calls=%fused_computation.1.clone.1 | convolution fusion | flops 158513152 | bytes 691040 | tf_op jit(solution)/shard_map/while/body/eval_jaxpr/qtc,jsc->qtjs/dot_general | solution.py:14
  54.8 1.5 %select_reduce_fusion.2 = f32[8,32,8]{1,2,0:T(8,128)S(1)} fusion(pred[8,300]{1,0:T(8,128)(4,1)S(1)} %get-tuple-element.105, bf16[8,300,128]{2,1,0:T(8,128)(2,1)S(1)} %get-tuple-element.107, bf16[16,8,32,128]{3,2,1,0:T(8,128)(2,1)} %get-tuple-element.106, s32[]{:T(128)} %get-tuple-element.96), kind=kOutput, calls=%fused_computation.1.clone.1 | convolution fusion | flops 158513152 | bytes 691040 | tf_op jit(solution)/shard_map/while/body/eval_jaxpr/qtc,jsc->qtjs/dot_general | solution.py:14
  56.4 1.5 %select_reduce_fusion.2 = f32[8,32,8]{1,2,0:T(8,128)S(1)} fusion(pred[8,300]{1,0:T(8,128)(4,1)S(1)} %get-tuple-element.105, bf16[8,300,128]{2,1,0:T(8,128)(2,1)S(1)} %get-tuple-element.107, bf16[16,8,32,128]{3,2,1,0:T(8,128)(2,1)} %get-tuple-element.106, s32[]{:T(128)} %get-tuple-element.96), kind=kOutput, calls=%fused_computation.1.clone.1 | convolution fusion | flops 158513152 | bytes 691040 | tf_op jit(solution)/shard_map/while/body/eval_jaxpr/qtc,jsc->qtjs/dot_general | solution.py:14
  58.0 1.5 %select_reduce_fusion.2 = f32[8,32,8]{1,2,0:T(8,128)S(1)} fusion(pred[8,300]{1,0:T(8,128)(4,1)S(1)} %get-tuple-element.105, bf16[8,300,128]{2,1,0:T(8,128)(2,1)S(1)} %get-tuple-element.107, bf16[16,8,32,128]{3,2,1,0:T(8,128)(2,1)} %get-tuple-element.106, s32[]{:T(128)} %get-tuple-element.96), kind=kOutput, calls=%fused_computation.1.clone.1 | convolution fusion | flops 158513152 | bytes 691040 | tf_op jit(solution)/shard_map/while/body/eval_jaxpr/qtc,jsc->qtjs/dot_general | solution.py:14
  59.6 1.5 %select_reduce_fusion.2 = f32[8,32,8]{1,2,0:T(8,128)S(1)} fusion(pred[8,300]{1,0:T(8,128)(4,1)S(1)} %get-tuple-element.105, bf16[8,300,128]{2,1,0:T(8,128)(2,1)S(1)} %get-tuple-element.107, bf16[16,8,32,128]{3,2,1,0:T(8,128)(2,1)} %get-tuple-element.106, s32[]{:T(128)} %get-tuple-element.96), kind=kOutput, calls=%fused_computation.1.clone.1 | convolution fusion | flops 158513152 | bytes 691040 | tf_op jit(solution)/shard_map/while/body/eval_jaxpr/qtc,jsc->qtjs/dot_general | solution.py:14
  61.2 1.5 %select_reduce_fusion.2 = f32[8,32,8]{1,2,0:T(8,128)S(1)} fusion(pred[8,300]{1,0:T(8,128)(4,1)S(1)} %get-tuple-element.105, bf16[8,300,128]{2,1,0:T(8,128)(2,1)S(1)} %get-tuple-element.107, bf16[16,8,32,128]{3,2,1,0:T(8,128)(2,1)} %get-tuple-element.106, s32[]{:T(128)} %get-tuple-element.96), kind=kOutput, calls=%fused_computation.1.clone.1 | convolution fusion | flops 158513152 | bytes 691040 | tf_op jit(solution)/shard_map/while/body/eval_jaxpr/qtc,jsc->qtjs/dot_general | solution.py:14
  62.8 1.5 %select_reduce_fusion.2 = f32[8,32,8]{1,2,0:T(8,128)S(1)} fusion(pred[8,300]{1,0:T(8,128)(4,1)S(1)} %get-tuple-element.105, bf16[8,300,128]{2,1,0:T(8,128)(2,1)S(1)} %get-tuple-element.107, bf16[16,8,32,128]{3,2,1,0:T(8,128)(2,1)} %get-tuple-element.106, s32[]{:T(128)} %get-tuple-element.96), kind=kOutput, calls=%fused_computation.1.clone.1 | convolution fusion | flops 158513152 | bytes 691040 | tf_op jit(solution)/shard_map/while/body/eval_jaxpr/qtc,jsc->qtjs/dot_general | solution.py:14
  64.4 1.5 %select_reduce_fusion.2 = f32[8,32,8]{1,2,0:T(8,128)S(1)} fusion(pred[8,300]{1,0:T(8,128)(4,1)S(1)} %get-tuple-element.105, bf16[8,300,128]{2,1,0:T(8,128)(2,1)S(1)} %get-tuple-element.107, bf16[16,8,32,128]{3,2,1,0:T(8,128)(2,1)} %get-tuple-element.106, s32[]{:T(128)} %get-tuple-element.96), kind=kOutput, calls=%fused_computation.1.clone.1 | convolution fusion | flops 158513152 | bytes 691040 | tf_op jit(solution)/shard_map/while/body/eval_jaxpr/qtc,jsc->qtjs/dot_general | solution.py:14
  66.0 1.5 %select_reduce_fusion.2 = f32[8,32,8]{1,2,0:T(8,128)S(1)} fusion(pred[8,300]{1,0:T(8,128)(4,1)S(1)} %get-tuple-element.105, bf16[8,300,128]{2,1,0:T(8,128)(2,1)S(1)} %get-tuple-element.107, bf16[16,8,32,128]{3,2,1,0:T(8,128)(2,1)} %get-tuple-element.106, s32[]{:T(128)} %get-tuple-element.96), kind=kOutput, calls=%fused_computation.1.clone.1 | convolution fusion | flops 158513152 | bytes 691040 | tf_op jit(solution)/shard_map/while/body/eval_jaxpr/qtc,jsc->qtjs/dot_general | solution.py:14
  67.5 1.5 %select_reduce_fusion.2 = f32[8,32,8]{1,2,0:T(8,128)S(1)} fusion(pred[8,300]{1,0:T(8,128)(4,1)S(1)} %get-tuple-element.105, bf16[8,300,128]{2,1,0:T(8,128)(2,1)S(1)} %get-tuple-element.107, bf16[16,8,32,128]{3,2,1,0:T(8,128)(2,1)} %get-tuple-element.106, s32[]{:T(128)} %get-tuple-element.96), kind=kOutput, calls=%fused_computation.1.clone.1 | convolution fusion | flops 158513152 | bytes 691040 | tf_op jit(solution)/shard_map/while/body/eval_jaxpr/qtc,jsc->qtjs/dot_general | solution.py:14
  69.1 1.5 %select_reduce_fusion.2 = f32[8,32,8]{1,2,0:T(8,128)S(1)} fusion(pred[8,300]{1,0:T(8,128)(4,1)S(1)} %get-tuple-element.105, bf16[8,300,128]{2,1,0:T(8,128)(2,1)S(1)} %get-tuple-element.107, bf16[16,8,32,128]{3,2,1,0:T(8,128)(2,1)} %get-tuple-element.106, s32[]{:T(128)} %get-tuple-element.96), kind=kOutput, calls=%fused_computation.1.clone.1 | convolution fusion | flops 158513152 | bytes 691040 | tf_op jit(solution)/shard_map/while/body/eval_jaxpr/qtc,jsc->qtjs/dot_general | solution.py:14
  70.7 1.5 %select_reduce_fusion.2 = f32[8,32,8]{1,2,0:T(8,128)S(1)} fusion(pred[8,300]{1,0:T(8,128)(4,1)S(1)} %get-tuple-element.105, bf16[8,300,128]{2,1,0:T(8,128)(2,1)S(1)} %get-tuple-element.107, bf16[16,8,32,128]{3,2,1,0:T(8,128)(2,1)} %get-tuple-element.106, s32[]{:T(128)} %get-tuple-element.96), kind=kOutput, calls=%fused_computation.1.clone.1 | convolution fusion | flops 158513152 | bytes 691040 | tf_op jit(solution)/shard_map/while/body/eval_jaxpr/qtc,jsc->qtjs/dot_general | solution.py:14
  72.5 6.3 %all_to_all.10 = f32[4,1,256]{2,1,0:T(1,128)S(1)} all-to-all(f32[4,1,256]{2,1,0:T(1,128)S(1)} %reshape.52), channel_id=1, replica_groups=mesh['replica'=2,'data2'=4,'data'=4] {'data'}, dimensions={0} | all-to-all | bytes 8192 | tf_op jit(solution)/shard_map/all_to_all | solution.py:40
  79.3 0.7 reduce.4
  80.2 0.7 reshape.54
  80.9 3.2 %all-to-all-start.1 = ((f32[4,1,256]{2,1,0:T(1,128)}), f32[4,1,256]{2,1,0:T(1,128)S(1)}, u32[]{:S(2)}, u32[]{:S(2)}) async-start(f32[4,1,256]{2,1,0:T(1,128)} %reshape.54), calls=%async_computation.1 | async-start | bytes 8192 | tf_op jit(solution)/shard_map/all_to_all | solution.py:41
  84.8 4.7 %all-to-all-done.1 = f32[4,1,256]{2,1,0:T(1,128)S(1)} async-done(((f32[4,1,256]{2,1,0:T(1,128)}), f32[4,1,256]{2,1,0:T(1,128)S(1)}, u32[]{:S(2)}, u32[]{:S(2)}) %all-to-all-start.1) | async-done | bytes 4128 | tf_op jit(solution)/shard_map/all_to_all | solution.py:41
  89.5 0.7 reduce.5
  90.9 0.6 gather_fusion
  91.5 1.1 fusion.9
  92.7 30.1 %psum.7 = f32[]{:T(128)} all-reduce(f32[]{:T(128)} %get-tuple-element.50), channel_id=1, replica_groups=mesh['replica'=2,'data2'=4,'data'=4] {'data2','data'}, use_global_device_ids=true, to_apply=%region_9.10 | all-reduce | flops 1 | bytes 8 | tf_op jit(solution)/shard_map/psum | solution.py:47
  (57 shorter events, 3.7 us)
Async XLA Ops:
  7.2 1.0 copy-start
  7.2 39.7 %all-gather.2.cloned.1.call-start = ((), (), s32[]{:S(2)}) async-start(), calls=%async_computation.2 | async-start | bytes 1310720 | tf_op jit(solution)/shard_map/all_gather | solution.py:36
  17.6 3.8 %copy-start.1 = (s32[8,300]{1,0:T(8,128)S(1)}, s32[8,300]{1,0:T(8,128)}, u32[]{:S(2)}) copy-start(s32[8,300]{1,0:T(8,128)} %param.12) | copy-start | bytes 28804
  80.9 8.6 %all-to-all-start.1 = ((f32[4,1,256]{2,1,0:T(1,128)}), f32[4,1,256]{2,1,0:T(1,128)S(1)}, u32[]{:S(2)}, u32[]{:S(2)}) async-start(f32[4,1,256]{2,1,0:T(1,128)} %reshape.54), calls=%async_computation.1 | async-start | bytes 8192 | tf_op jit(solution)/shard_map/all_to_all | solution.py:41
Sparse Core Ops, SparseCore 0:
  17.7 29.1 all-gather.1
where the time goes:
time: 132 us; the launch traced here: 131 us
  blocking collectives  43.7 us (33%)
  waiting for transfers between devices  30.1 us (23%)
  matrix products  28.4 us (22%)
  between operations  16.6 us (13%)
  other arithmetic  5.46 us (4%)
  local copies, waits for them, and re-layouts  3.63 us (3%)
  starting transfers between devices  3.28 us (2%)
    psum x1, blocking collectives, local_step(): mean_loss = lax.psum(jnp.sum(losses), batch_axes) / total_batch  30.1 us
    all_gather x1, waiting for transfers between devices, local_step(): q_all = lax.all_gather(q_all, 'data2', axis=0, tiled=True)  25.4 us
    dot_general x16, matrix products, tile_scores(): jnp.einsum('qtc,jsc->qtjs', q_block, p_block, preferred_element_type=jnp....  23.9 us
    all_gather x1, blocking collectives, local_step(): q_all = lax.all_gather(q_vecs, 'data', axis=0, tiled=True)  7.28 us
    all_to_all x1, blocking collectives, local_step(): column = lax.all_to_all(column, 'data', 1, 1, tiled=True)  6.34 us
    all_to_all x1, waiting for transfers between devices, local_step(): column = lax.all_to_all(column, 'data2', 0, 0, tiled=True)  4.67 us
    dot_general x2, matrix products, project_norm(): jnp.einsum('bld,de->ble', hidden, w_proj, preferred_element_type=jnp.floa...  4.52 us
    all_to_all x1, starting transfers between devices, local_step(): column = lax.all_to_all(column, 'data2', 0, 0, tiled=True)  3.24 us
  transfers between devices with their start and end apart: 2, of which 2 were waited for; matrix products, arithmetic and copies ran while one was open for 3% of the time, Pallas kernels for 0%

commit v1 on v0

v1 whole, which is shorter than its diff:
```python
import functools

import jax
import jax.numpy as jnp
from jax import lax
from jax.experimental import pallas as pl
from jax.experimental.pallas import tpu as pltpu
from jax.sharding import PartitionSpec as P

F32 = jnp.float32
BF16 = jnp.bfloat16
LANES = 128
BIG = 1e30


def inv_norm(x, axis):
    return lax.rsqrt(jnp.maximum(jnp.sum(x * x, axis=axis, keepdims=True), 1e-24))


def iota(shape, dim):
    return lax.broadcasted_iota(jnp.int32, shape, dim)


def kernel(dims, q_hbm, d_hbm, w_hbm, qm_hbm, dm_hbm, t_hbm, loss_ref, mean_ref,
           qh, dh, w, qm, dm, temp, dmp, pa, qb, bm, st,
           in_sem, doc_sem, send_sem, recv_sem, ssend_sem, srecv_sem):
    nz, ny, nb, qlen, dlen, drow, hidden = dims
    group = nz * ny * 2
    qtok = nb * qlen
    z = lax.axis_index('data2')
    yc = lax.axis_index('data')
    y = yc // 2
    c = yc % 2
    me = z * (2 * ny) + yc

    def dev(zz, yy, cc):
        return {'data2': zz, 'data': yy * 2 + cc}

    def bid(zz, yy, cc):
        return zz * (2 * ny) + yy * 2 + cc

    oy, oc = 1 - y, 1 - c
    zx = (z + 1 - 2 * (z % 2), (z + 2) % 4, 3 - z)

    loads = [
        pltpu.make_async_copy(qm_hbm, qm, in_sem.at[0]),
        pltpu.make_async_copy(w_hbm, w, in_sem.at[1]),
        pltpu.make_async_copy(q_hbm, qh, in_sem.at[2]),
        pltpu.make_async_copy(dm_hbm, dm, in_sem.at[3]),
        pltpu.make_async_copy(t_hbm, temp, in_sem.at[4]),
    ]
    for cp in loads:
        cp.start()
    docs = [pltpu.make_async_copy(d_hbm.at[j], dh.at[j], doc_sem.at[j]) for j in range(nb)]
    for cp in docs:
        cp.start()

    barrier = pltpu.get_barrier_semaphore()
    near = [dev(z, y, oc), dev(z, oy, c)] + [dev(k, y, c) for k in zx]
    for d in near:
        pl.semaphore_signal(barrier, inc=1, device_id=d, device_id_type=pl.DeviceIdType.MESH)

    loads[0].wait()
    spread = (iota((qlen, qtok), 1) % qlen == iota((qlen, qtok), 0)).astype(BF16)
    qmf = jnp.dot(qm[...].astype(F32).astype(BF16), spread, preferred_element_type=F32)
    own_row = iota((nb, qtok), 1) // qlen == iota((nb, qtok), 0)
    qmask = jnp.sum(jnp.where(own_row, qmf, 0.0), axis=0, keepdims=True)
    loads[1].wait()
    loads[2].wait()
    qp = jnp.dot(qh[...].reshape(qtok, hidden), w[...], preferred_element_type=F32)
    qt = qp.T
    qt = qt * inv_norm(qt, 0)
    qb[me] = jnp.where(qmask > 0, qt, 0.0).astype(BF16)

    pl.semaphore_wait(barrier, len(near))

    sends = []

    def send(block, d):
        k = len(sends)
        cp = pltpu.make_async_remote_copy(
            src_ref=qb.at[block], dst_ref=qb.at[block], send_sem=send_sem.at[k],
            recv_sem=recv_sem.at[block], device_id=d, device_id_type=pl.DeviceIdType.MESH)
        cp.start()
        sends.append(cp)

    def arrive(block):
        pltpu.make_async_remote_copy(
            src_ref=qb.at[block], dst_ref=qb.at[block], send_sem=send_sem.at[0],
            recv_sem=recv_sem.at[block], device_id=dev(z, y, oc),
            device_id_type=pl.DeviceIdType.MESH).wait_recv()

    to_core, to_y = dev(z, y, oc), dev(z, oy, c)
    for k in zx:
        send(me, dev(k, y, c))
    send(me, to_y)
    send(me, to_core)

    loads[3].wait()
    dmp[...] = jnp.full(dmp.shape, -1.0, F32)
    dmp[:, pl.ds(0, dlen)] = dm[...].astype(F32) - 1.0
    pick = jnp.where(iota((nb, nb * LANES), 1) == iota((nb, nb * LANES), 0) * LANES, BIG, 0.0)
    bias = lax.dot_general(dmp[...], pick, (((0,), (0,)), ((), ())), preferred_element_type=F32)
    for j in range(nb):
        pa[pl.ds(j * drow, drow), pl.ds(LANES, LANES)] = (
            bias[:drow, j * LANES:(j + 1) * LANES].astype(BF16))
    for j in range(nb):
        pa[pl.ds((j + 1) * drow - 16, 16), pl.ds(0, LANES)] = jnp.zeros((16, LANES), BF16)
        docs[j].wait()
        dp = jnp.dot(dh[j], w[...], preferred_element_type=F32)
        pa[pl.ds(j * drow, dlen), pl.ds(0, LANES)] = (dp * inv_norm(dp, 1)).astype(BF16)

    ones_row = (iota((LANES, qtok), 0) == 0).astype(BF16)

    def score(block):
        rhs = jnp.concatenate([qb[block], ones_row], axis=0)
        sim = jnp.dot(pa[...], rhs, preferred_element_type=F32)
        bm[block] = jnp.max(sim.reshape(nb, drow, qtok), axis=1)

    def step(block, fwd=()):
        arrive(block)
        for d in fwd:
            send(block, d)
        score(block)

    score(me)
    step(bid(z, y, oc))
    step(bid(z, oy, c), (to_core,))
    step(bid(zx[0], y, c), (to_y, to_core))
    step(bid(z, oy, oc))
    step(bid(zx[1], y, c), (to_y, to_core))
    step(bid(zx[0], y, oc))
    step(bid(zx[0], oy, c), (to_core,))
    step(bid(zx[2], y, c), (to_y, to_core))
    step(bid(zx[1], y, oc))
    step(bid(zx[1], oy, c), (to_core,))
    step(bid(zx[0], oy, oc))
    step(bid(zx[2], y, oc))
    step(bid(zx[2], oy, c), (to_core,))
    step(bid(zx[1], oy, oc))
    step(bid(zx[2], oy, oc))

    best = bm[...].reshape(group * nb, qtok)
    sel = (iota((qtok, LANES), 0) // qlen == iota((qtok, LANES), 1) % nb).astype(BF16)
    hi = best.astype(BF16)
    rest = best - hi.astype(F32)
    mid = rest.astype(BF16)
    low = (rest - mid.astype(F32)).astype(BF16)
    tot = (jnp.dot(low, sel, preferred_element_type=F32)
           + jnp.dot(mid, sel, preferred_element_type=F32)
           + jnp.dot(hi, sel, preferred_element_type=F32))
    tot = tot.reshape(group, nb, LANES)
    here = iota((group, nb, LANES), 2) // nb == iota((group, nb, LANES), 0)
    scores = jnp.sum(jnp.where(here, tot, 0.0), axis=0)

    loads[4].wait()
    logits = scores / temp[0]
    top = jnp.max(logits, axis=0, keepdims=True)
    part = jnp.sum(jnp.exp(logits - top), axis=0, keepdims=True)
    mine = iota((nb, LANES), 1) == me * nb + iota((nb, LANES), 0)
    diag = jnp.sum(jnp.where(mine, logits, 0.0), axis=0, keepdims=True)
    st[me] = jnp.concatenate([top, part, diag, jnp.zeros_like(diag)], axis=0)

    stats = []
    for k in range(1, group):
        peer = (me + k) % group
        cp = pltpu.make_async_remote_copy(
            src_ref=st.at[me], dst_ref=st.at[me], send_sem=ssend_sem.at[k],
            recv_sem=srecv_sem.at[me],
            device_id={'data2': peer // (2 * ny), 'data': peer % (2 * ny)},
            device_id_type=pl.DeviceIdType.MESH)
        cp.start()
        stats.append(cp)
    for k in range(1, group):
        peer = (me + k) % group
        pltpu.make_async_remote_copy(
            src_ref=st.at[peer], dst_ref=st.at[peer], send_sem=ssend_sem.at[0],
            recv_sem=srecv_sem.at[peer], device_id=dev(z, y, oc),
            device_id_type=pl.DeviceIdType.MESH).wait_recv()

    tops = st[:, 0, :]
    best_top = jnp.max(tops, axis=0, keepdims=True)
    total = jnp.sum(st[:, 1, :] * jnp.exp(tops - best_top), axis=0, keepdims=True)
    losses = best_top + jnp.log(total) - jnp.sum(st[:, 2, :], axis=0, keepdims=True)
    mean_ref[...] = jnp.sum(losses, axis=1, keepdims=True) / (group * nb)
    moved = pltpu.roll(jnp.broadcast_to(losses, (8, LANES)), (LANES - me * nb) % LANES, 1)
    loss_ref[...] = moved[0:1, 0:nb]
    for cp in sends:
        cp.wait_send()
    for cp in stats:
        cp.wait_send()


def solution(mesh):
    nz, nd = mesh.shape['data2'], mesh.shape['data']
    ny = nd // 2
    group = nz * nd
    row_spec = P(('replica', 'data2', 'data'))
    tok_spec = P(('replica', 'data2', 'data'), None, None)
    mask_spec = P(('replica', 'data2', 'data'), None)

    def local_step(qh, dh, w, qm, dm, temp):
        nb, qlen, hidden = qh.shape
        dlen = dh.shape[1]
        drow = -(-dlen // 16) * 16
        dpad = -(-dlen // LANES) * LANES
        dims = (nz, ny, nb, qlen, dlen, drow, hidden)
        losses, mean = pl.pallas_call(
            functools.partial(kernel, dims),
            out_shape=(jax.ShapeDtypeStruct((1, nb), F32), jax.ShapeDtypeStruct((1, 1), F32)),
            in_specs=[pl.BlockSpec(memory_space=pl.ANY)] * 6,
            out_specs=(pl.BlockSpec(memory_space=pltpu.VMEM), pl.BlockSpec(memory_space=pltpu.VMEM)),
            scratch_shapes=[
                pltpu.VMEM((nb, qlen, hidden), BF16),
                pltpu.VMEM((nb, dlen, hidden), BF16),
                pltpu.VMEM(w.shape, BF16),
                pltpu.VMEM((nb, qlen), jnp.int32),
                pltpu.VMEM((nb, dlen), jnp.int32),
                pltpu.SMEM((1,), F32),
                pltpu.VMEM((nb, dpad), F32),
                pltpu.VMEM((nb * drow, 2 * LANES), BF16),
                pltpu.VMEM((group, LANES, nb * qlen), BF16),
                pltpu.VMEM((group, nb, nb * qlen), F32),
                pltpu.VMEM((group, 4, LANES), F32),
                pltpu.SemaphoreType.DMA((5,)),
                pltpu.SemaphoreType.DMA((nb,)),
                pltpu.SemaphoreType.DMA((group,)),
                pltpu.SemaphoreType.DMA((group,)),
                pltpu.SemaphoreType.DMA((group,)),
                pltpu.SemaphoreType.DMA((group,)),
            ],
            compiler_params=pltpu.CompilerParams(collective_id=0, has_side_effects=True),
            name='late_interaction',
        )(qh, dh, w, qm, dm, temp.reshape(1))
        return losses.reshape(nb), mean.reshape(1)

    return jax.shard_map(
        local_step, mesh=mesh,
        in_specs=(tok_spec, tok_spec, P(None, None), mask_spec, mask_spec, P()),
        out_specs=(row_spec, P('replica')), check_vma=False)
```

time: 132 us -> 36.9 us (0.28)
  blocking collectives: 43.7 us -> 0 us
  waiting for transfers between devices: 30.1 us -> 0 us
  matrix products: 28.4 us -> 0 us
  Pallas kernels: 0 us -> 27.9 us
  between operations: 16.6 us -> 2.96 us
  other arithmetic: 5.46 us -> 0 us
  starting transfers between devices: 3.28 us -> 0 us
  local copies, waits for them, and re-layouts: 3.63 us -> 5.76 us
    psum x1 -> x0, blocking collectives: 30.1 us -> none  [local_step(): mean_loss = lax.psum(jnp.sum(losses), batch_axes) / total_batch]
    dot_general x18 -> x0, matrix products: 28.4 us -> none  [the longest x16 23.9 us: tile_scores(): jnp.einsum('qtc,jsc->qtjs', q_block, p_block, preferred_element_type=jnp....]
    pallas_call x0 -> x1, Pallas kernels: none -> 27.9 us  [local_step(): pl.pallas_call(functools.partial(kernel, dims), out_shape=(jax.ShapeDtype...]
    all_gather x1 -> x0, waiting for transfers between devices: 25.4 us -> none  [local_step(): q_all = lax.all_gather(q_all, 'data2', axis=0, tiled=True)]
    all_gather x1 -> x0, blocking collectives: 7.28 us -> none  [local_step(): q_all = lax.all_gather(q_vecs, 'data', axis=0, tiled=True)]
    all_to_all x1 -> x0, blocking collectives: 6.34 us -> none  [local_step(): column = lax.all_to_all(column, 'data', 1, 1, tiled=True)]
    all_to_all x1 -> x0, waiting for transfers between devices: 4.67 us -> none  [local_step(): column = lax.all_to_all(column, 'data2', 0, 0, tiled=True)]
    unnamed x8 -> x2, local copies, waits for them, and re-layouts: 2.04 us -> 5.76 us
  transfers between devices with their start and end apart: 2 -> 0, of which waited for: 2 -> 0; matrix products, arithmetic and copies ran while one was open for 3% -> 0% of each run, Pallas kernels for 0% -> 0%
where the time goes in v1:
time: 36.9 us; the launch traced here: 36.7 us
  Pallas kernels  27.9 us (76%)
  local copies, waits for them, and re-layouts  5.76 us (16%)
  between operations  2.96 us (8%)
    pallas_call x1, Pallas kernels, local_step(): pl.pallas_call(functools.partial(kernel, dims), out_shape=(jax.ShapeDtype...  27.9 us
    unnamed x2, local copies, waits for them, and re-layouts  5.76 us

profile of v1, /device:TPU:0, one launch (start us, length us, event | category | flops | bytes accessed | tf_op | source)
XLA Modules:
  0.0 36.7 jit_solution(12575685926482564550)
XLA Ops:
  1.3 4.6 %copy.8.d_hbm = bf16[8,300,768]{2,1,0:T(8,128)(2,1)} copy(bf16[8,300,768]{2,0,1:T(8,128)(2,1)} %param.7) | data formatting | bytes 7372800 | tf_op args[1]
  5.8 27.9 %late_interaction.1 = (f32[1,8]{1,0:T(1,128)}, f32[1,1]{1,0:T(1,128)}) custom-call(bf16[8,32,768]{2,1,0:T(8,128)(2,1)} %q_hbm.1, bf16[8,300,768]{2,1,0:T(8,128)(2,1)} %copy.8.d_hbm, bf16[768,128]{1,0:T(8,128)(2,1)} %w_hbm.1, s32[8,32]{1,0:T(8,128)} %qm_hbm.1, s32[8,300]{1,0:T(8,128)} %dm_hbm.1, f32[1]{0:T(128)} %bitcast.3.t_hbm), custom_call_target="tpu_custom_call" | custom-call | tf_op jit(solution)/shard_map/late_interaction/pallas_call | solution.py:208
  33.8 1.2 %copy.12 = f32[8]{0:T(128)} copy(f32[8]{0:T(128)} %bitcast.4) | data formatting | bytes 64

commit v2 on v1

--- a/solution.py
+++ b/solution.py
@@ -21,10 +21,11 @@
     return lax.broadcasted_iota(jnp.int32, shape, dim)
 
 
-def kernel(dims, q_hbm, d_hbm, w_hbm, qm_hbm, dm_hbm, t_hbm, loss_ref, mean_ref,
-           qh, dh, w, qm, dm, temp, dmp, pa, qb, bm, st,
+def kernel(dims, q_hbm, d_hbm, w_hbm, qm_hbm, dm_hbm, t_hbm, out_ref,
+           qh, dh, w, qm, dm, temp, pa, qb, bm, st,
            in_sem, doc_sem, send_sem, recv_sem, ssend_sem, srecv_sem):
-    nz, ny, nb, qlen, dlen, drow, hidden = dims
+    nz, ny, nb, qlen, dlen, parts, halves, hidden = dims
+    part = dlen * nb // parts
     group = nz * ny * 2
     qtok = nb * qlen
     z = lax.axis_index('data2')
@@ -51,7 +52,8 @@
     ]
     for cp in loads:
         cp.start()
-    docs = [pltpu.make_async_copy(d_hbm.at[j], dh.at[j], doc_sem.at[j]) for j in range(nb)]
+    docs = [pltpu.make_async_copy(d_hbm.at[pl.ds(j * part, part)], dh.at[pl.ds(j * part, part)],
+                                  doc_sem.at[j]) for j in range(parts)]
     for cp in docs:
         cp.start()
 
@@ -75,70 +77,83 @@
     pl.semaphore_wait(barrier, len(near))
 
     sends = []
-
-    def send(block, d):
-        k = len(sends)
-        cp = pltpu.make_async_remote_copy(
-            src_ref=qb.at[block], dst_ref=qb.at[block], send_sem=send_sem.at[k],
-            recv_sem=recv_sem.at[block], device_id=d, device_id_type=pl.DeviceIdType.MESH)
+    piece = LANES // halves
+
+    def move(block, h, d, k):
+        view = qb.at[block, pl.ds(h * piece, piece)]
+        return pltpu.make_async_remote_copy(
+            src_ref=view, dst_ref=view, send_sem=send_sem.at[k], recv_sem=recv_sem.at[block, h],
+            device_id=d, device_id_type=pl.DeviceIdType.MESH)
+
+    def send(block, h, d):
+        cp = move(block, h, d, len(sends))
         cp.start()
         sends.append(cp)
 
-    def arrive(block):
-        pltpu.make_async_remote_copy(
-            src_ref=qb.at[block], dst_ref=qb.at[block], send_sem=send_sem.at[0],
-            recv_sem=recv_sem.at[block], device_id=dev(z, y, oc),
-            device_id_type=pl.DeviceIdType.MESH).wait_recv()
+    def arrive(block, fwd=()):
+        for h in range(halves):
+            move(block, h, to_core, 0).wait_recv()
+            for d in fwd:
+                send(block, h, d)
 
     to_core, to_y = dev(z, y, oc), dev(z, oy, c)
-    for k in zx:
-        send(me, dev(k, y, c))
-    send(me, to_y)
-    send(me, to_core)
+    for d in [dev(zx[0], y, c), to_y, dev(zx[1], y, c), dev(zx[2], y, c), to_core]:
+        for h in range(halves):
+            send(me, h, d)
 
     loads[3].wait()
-    dmp[...] = jnp.full(dmp.shape, -1.0, F32)
-    dmp[:, pl.ds(0, dlen)] = dm[...].astype(F32) - 1.0
-    pick = jnp.where(iota((nb, nb * LANES), 1) == iota((nb, nb * LANES), 0) * LANES, BIG, 0.0)
-    bias = lax.dot_general(dmp[...], pick, (((0,), (0,)), ((), ())), preferred_element_type=F32)
-    for j in range(nb):
-        pa[pl.ds(j * drow, drow), pl.ds(LANES, LANES)] = (
-            bias[:drow, j * LANES:(j + 1) * LANES].astype(BF16))
-    for j in range(nb):
-        pa[pl.ds((j + 1) * drow - 16, 16), pl.ds(0, LANES)] = jnp.zeros((16, LANES), BF16)
-        docs[j].wait()
-        dp = jnp.dot(dh[j], w[...], preferred_element_type=F32)
-        pa[pl.ds(j * drow, dlen), pl.ds(0, LANES)] = (dp * inv_norm(dp, 1)).astype(BF16)
+    for cp in docs:
+        cp.wait()
+    bias = (dm[...].astype(F32) - 1.0) * BIG
+    for j in range(parts):
+        rows = pl.ds(j * part, part)
+        dp = jnp.dot(dh[rows], w[...], preferred_element_type=F32)
+        pa[rows, pl.ds(0, LANES)] = (dp * inv_norm(dp, 1)).astype(BF16)
+        for s in range(j * part // nb, (j + 1) * part // nb, 2):
+            pair = [jnp.broadcast_to(bias[:, k:k + 1], (nb, LANES)) for k in (s, s + 1)]
+            pa[pl.ds(s * nb, 2 * nb), pl.ds(LANES, LANES)] = jnp.concatenate(pair, axis=0).astype(BF16)
 
     ones_row = (iota((LANES, qtok), 0) == 0).astype(BF16)
 
     def score(block):
         rhs = jnp.concatenate([qb[block], ones_row], axis=0)
-        sim = jnp.dot(pa[...], rhs, preferred_element_type=F32)
-        bm[block] = jnp.max(sim.reshape(nb, drow, qtok), axis=1)
-
-    def step(block, fwd=()):
-        arrive(block)
-        for d in fwd:
-            send(block, d)
-        score(block)
-
+        half = dlen // 2
+        best = [jnp.max(jnp.dot(pa[pl.ds(k * half * nb, half * nb)], rhs, preferred_element_type=F32)
+                        .reshape(half, nb, qtok), axis=0) for k in range(2)]
+        bm[block] = jnp.maximum(best[0], best[1])
+
+    both = (to_y, to_core)
+    arrive(bid(z, oy, c), (to_core,))
+    arrive(bid(zx[0], y, c), both)
     score(me)
-    step(bid(z, y, oc))
-    step(bid(z, oy, c), (to_core,))
-    step(bid(zx[0], y, c), (to_y, to_core))
-    step(bid(z, oy, oc))
-    step(bid(zx[1], y, c), (to_y, to_core))
-    step(bid(zx[0], y, oc))
-    step(bid(zx[0], oy, c), (to_core,))
-    step(bid(zx[2], y, c), (to_y, to_core))
-    step(bid(zx[1], y, oc))
-    step(bid(zx[1], oy, c), (to_core,))
-    step(bid(zx[0], oy, oc))
-    step(bid(zx[2], y, oc))
-    step(bid(zx[2], oy, c), (to_core,))
-    step(bid(zx[1], oy, oc))
-    step(bid(zx[2], oy, oc))
+    arrive(bid(z, y, oc))
+    score(bid(z, y, oc))
+    score(bid(z, oy, c))
+    score(bid(zx[0], y, c))
+    arrive(bid(z, oy, oc))
+    score(bid(z, oy, oc))
+    arrive(bid(zx[0], oy, c), (to_core,))
+    arrive(bid(zx[0], y, oc))
+    score(bid(zx[0], y, oc))
+    arrive(bid(zx[1], y, c), both)
+    score(bid(zx[0], oy, c))
+    score(bid(zx[1], y, c))
+    arrive(bid(zx[0], oy, oc))
+    score(bid(zx[0], oy, oc))
+    arrive(bid(zx[1], y, oc))
+    arrive(bid(zx[2], y, c), both)
+    score(bid(zx[1], y, oc))
+    arrive(bid(zx[1], oy, c), (to_core,))
+    score(bid(zx[2], y, c))
+    score(bid(zx[1], oy, c))
+    arrive(bid(zx[2], y, oc))
+    score(bid(zx[2], y, oc))
+    arrive(bid(zx[1], oy, oc))
+    arrive(bid(zx[2], oy, c), (to_core,))
+    score(bid(zx[1], oy, oc))
+    score(bid(zx[2], oy, c))
+    arrive(bid(zx[2], oy, oc))
+    score(bid(zx[2], oy, oc))
 
     best = bm[...].reshape(group * nb, qtok)
     sel = (iota((qtok, LANES), 0) // qlen == iota((qtok, LANES), 1) % nb).astype(BF16)
@@ -182,9 +197,9 @@
     best_top = jnp.max(tops, axis=0, keepdims=True)
     total = jnp.sum(st[:, 1, :] * jnp.exp(tops - best_top), axis=0, keepdims=True)
     losses = best_top + jnp.log(total) - jnp.sum(st[:, 2, :], axis=0, keepdims=True)
-    mean_ref[...] = jnp.sum(losses, axis=1, keepdims=True) / (group * nb)
+    mean = jnp.sum(losses, axis=1, keepdims=True) / (group * nb)
     moved = pltpu.roll(jnp.broadcast_to(losses, (8, LANES)), (LANES - me * nb) % LANES, 1)
-    loss_ref[...] = moved[0:1, 0:nb]
+    out_ref[...] = jnp.where(iota((1, LANES), 1) < nb, moved[0:1], mean)
     for cp in sends:
         cp.wait_send()
     for cp in stats:
@@ -202,37 +217,37 @@
     def local_step(qh, dh, w, qm, dm, temp):
         nb, qlen, hidden = qh.shape
         dlen = dh.shape[1]
-        drow = -(-dlen // 16) * 16
-        dpad = -(-dlen // LANES) * LANES
-        dims = (nz, ny, nb, qlen, dlen, drow, hidden)
-        losses, mean = pl.pallas_call(
+        parts = 6
+        halves = 1
+        dims = (nz, ny, nb, qlen, dlen, parts, halves, hidden)
+        flat = jnp.transpose(dh, (1, 0, 2)).reshape(dlen * nb, hidden)
+        out = pl.pallas_call(
             functools.partial(kernel, dims),
-            out_shape=(jax.ShapeDtypeStruct((1, nb), F32), jax.ShapeDtypeStruct((1, 1), F32)),
+            out_shape=pltpu.VMEM((1, LANES), F32),
             in_specs=[pl.BlockSpec(memory_space=pl.ANY)] * 6,
-            out_specs=(pl.BlockSpec(memory_space=pltpu.VMEM), pl.BlockSpec(memory_space=pltpu.VMEM)),
+            out_specs=pl.BlockSpec(memory_space=pltpu.VMEM),
             scratch_shapes=[
                 pltpu.VMEM((nb, qlen, hidden), BF16),
-                pltpu.VMEM((nb, dlen, hidden), BF16),
+                pltpu.VMEM((dlen * nb, hidden), BF16),
                 pltpu.VMEM(w.shape, BF16),
                 pltpu.VMEM((nb, qlen), jnp.int32),
                 pltpu.VMEM((nb, dlen), jnp.int32),
                 pltpu.SMEM((1,), F32),
-                pltpu.VMEM((nb, dpad), F32),
-                pltpu.VMEM((nb * drow, 2 * LANES), BF16),
+                pltpu.VMEM((dlen * nb, 2 * LANES), BF16),
                 pltpu.VMEM((group, LANES, nb * qlen), BF16),
                 pltpu.VMEM((group, nb, nb * qlen), F32),
                 pltpu.VMEM((group, 4, LANES), F32),
                 pltpu.SemaphoreType.DMA((5,)),
-                pltpu.SemaphoreType.DMA((nb,)),
-                pltpu.SemaphoreType.DMA((group,)),
-                pltpu.SemaphoreType.DMA((group,)),
+                pltpu.SemaphoreType.DMA((parts,)),
+                pltpu.SemaphoreType.DMA((group * halves,)),
+                pltpu.SemaphoreType.DMA((group, halves)),
                 pltpu.SemaphoreType.DMA((group,)),
                 pltpu.SemaphoreType.DMA((group,)),
             ],
             compiler_params=pltpu.CompilerParams(collective_id=0, has_side_effects=True),
             name='late_interaction',
-        )(qh, dh, w, qm, dm, temp.reshape(1))
-        return losses.reshape(nb), mean.reshape(1)
+        )(qh, flat, w, qm, dm, temp.reshape(1))
+        return out[0, :nb], out[0, nb:nb + 1]
 
     return jax.shard_map(
         local_step, mesh=mesh,

time: 36.9 us -> 26.6 us (0.72)
  local copies, waits for them, and re-layouts: 5.76 us -> 1.09 us
  Pallas kernels: 27.9 us -> 24.1 us
  between operations: 2.96 us -> 1.29 us
    unnamed x2 -> x0, local copies, waits for them, and re-layouts: 5.76 us -> none
    pallas_call x1, Pallas kernels: 27.9 us -> 24.1 us  [local_step(): pl.pallas_call(functools.partial(kernel, dims), out_shape=pltpu.VMEM((1,...]
    slice x0 -> x1, local copies, waits for them, and re-layouts: none -> 0.58 us  [local_step(): return (out[0, :nb], out[0, nb:nb + 1])]
    squeeze x0 -> x1, local copies, waits for them, and re-layouts: none -> 0.51 us  [local_step(): return (out[0, :nb], out[0, nb:nb + 1])]
where the time goes in v2:
time: 26.6 us; the launch traced here: 26.5 us
  Pallas kernels  24.1 us (91%)
  between operations  1.29 us (5%)
  local copies, waits for them, and re-layouts  1.09 us (4%)
    pallas_call x1, Pallas kernels, local_step(): pl.pallas_call(functools.partial(kernel, dims), out_shape=pltpu.VMEM((1,...  24.1 us
    slice x1, local copies, waits for them, and re-layouts, local_step(): return (out[0, :nb], out[0, nb:nb + 1])  0.58 us

profile of v2, /device:TPU:0, one launch (start us, length us, event | category | flops | bytes accessed | tf_op | source)
XLA Modules:
  0.0 26.5 jit_solution(15763247877043280029)
XLA Ops:
  1.3 24.1 %late_interaction.1 = f32[1,128]{1,0:T(1,128)S(1)} custom-call(bf16[8,32,768]{2,1,0:T(8,128)(2,1)} %q_hbm.1, bf16[2400,768]{1,0:T(8,128)(2,1)} %bitcast.8, bf16[768,128]{1,0:T(8,128)(2,1)} %w_hbm.1, s32[8,32]{1,0:T(8,128)} %qm_hbm.1, s32[8,300]{1,0:T(8,128)} %dm_hbm.1, f32[1]{0:T(128)} %bitcast.7.t_hbm), custom_call_target="tpu_custom_call" | custom-call | tf_op jit(solution)/shard_map/late_interaction/pallas_call | solution.py:224
  25.4 0.6 %slice.7 = f32[1,1]{1,0:T(1,128)} slice(f32[1,128]{1,0:T(1,128)S(1)} %late_interaction.1), slice={[0:1], [8:9]} | slice | bytes 8 | tf_op jit(solution)/shard_map/slice | solution.py:250
  26.0 0.5 %slice_bitcast_fusion = f32[8]{0:T(128)} fusion(f32[1,128]{1,0:T(1,128)S(1)} %late_interaction.1), kind=kLoop, calls=%fused_computation | loop fusion | bytes 64 | tf_op jit(solution)/shard_map/squeeze | solution.py:250
